TPU v7x, 32 devices: a whole 2x2x4 slice. The times are simulated.
32 devices in a mesh: expert: 4 (over x, core), shard: 8 (over z, y).
Axes of the slice: x: 2, y: 2, z: 4, core: 2. Of those that a mesh axis runs over, the one named last changes fastest.
Arguments:
- tokens: bfloat16 [48, 4096], P('shard', 'expert'), may hold values from -6 to 6
- expert_ids: int32 [48, 2], P('shard'), may hold values from 0 to 3, all different within a row; in each aligned block of 6 rows (0 to 5, 6 to 11, ...) at most 6 rows name the same one
- gates: float32 [48, 2], P('shard'), may hold values from 0.1 to 1
- gate_proj: bfloat16 [4, 4096, 8192], P('expert', None, 'shard'), may hold values from -0.09375 to 0.09375
- up_proj: bfloat16 [4, 4096, 8192], P('expert', None, 'shard'), may hold values from -0.09375 to 0.09375
- down_proj_t: bfloat16 [4, 4096, 8192], P('expert', 'shard'), may hold values from -0.0625 to 0.0625
Outputs:
- mixed: bfloat16 [48, 4096], P('shard', 'expert')
Inputs may be any that keep to these rules, and one draw needn't show every extreme that they name: `expert_ids`: each token names two different experts; among the 6 tokens of one aligned block no expert is named more than 6 times, and in every draw some expert is named exactly 6 times in some block.
All inputs are finite; a program needn't handle non-finite values.
Results may differ from a plain program's by a relative error of at most 0.0085.
Values may be sent and summed in bfloat16 or wider, within the bound.
A program may use at most 64 MiB of HBM per device.

v0:
```python
import jax
import jax.numpy as jnp
from jax import lax
from jax.sharding import PartitionSpec as P


def shards(tokens, expert_ids, gates, gate_proj, up_proj, down_proj_t):
    experts = lax.axis_size("expert")
    own_expert = lax.axis_index("expert")
    tok_count = tokens.shape[0]
    capacity = min(tok_count, 4 * tok_count // experts)
    expert_range = jnp.arange(experts, dtype=jnp.int32)
    matches = expert_ids[:, :, None] == expert_range[None, None, :]
    routed = jnp.sum(matches.astype(jnp.int32), axis=1)
    weight = jnp.sum(gates[:, :, None] * matches.astype(jnp.float32), axis=1)
    slot_rank = jnp.cumsum(routed, axis=0) - routed
    slot_range = jnp.arange(capacity, dtype=jnp.int32)
    selector = (slot_rank.T[:, None, :] == slot_range[None, :, None]) & (routed.T[:, None, :] > 0)
    selector_bf = selector.astype(jnp.bfloat16)
    whole = lax.all_gather(tokens, "expert", axis=1, tiled=True)
    own_select = lax.dynamic_index_in_dim(selector_bf, own_expert, 0, keepdims=False)
    own_rows = jnp.dot(own_select, whole, preferred_element_type=jnp.float32).astype(jnp.bfloat16)
    gate_local = gate_proj[0]
    up_local = up_proj[0]
    down_local = down_proj_t[0]
    piece = lax.all_gather(own_rows, "shard", axis=0, tiled=True)
    gate_out = jnp.dot(piece, gate_local, preferred_element_type=jnp.float32)
    up_out = jnp.dot(piece, up_local, preferred_element_type=jnp.float32)
    hidden = (jax.nn.silu(gate_out) * up_out).astype(jnp.bfloat16)
    out_columns = lax.dot_general(
        lax.all_gather(hidden, "shard", axis=1, tiled=True),
        down_local,
        (((1,), (1,)), ((), ())),
        preferred_element_type=jnp.float32,
    )
    expert_out = lax.all_to_all(
        out_columns.astype(jnp.bfloat16), "shard", split_axis=0, concat_axis=1, tiled=True
    )
    gathered_out = lax.all_to_all(expert_out, "expert", split_axis=1, concat_axis=0, tiled=True)
    combiner = (
        (selector.astype(jnp.float32) * weight.T[:, None, :])
        .reshape(experts * capacity, tok_count)
        .T
    )
    mixed_sum = jnp.dot(combiner, gathered_out.astype(jnp.float32), precision=lax.Precision.HIGHEST)
    return mixed_sum.astype(jnp.bfloat16)


def solution(mesh):
    in_specs = (
        P("shard", "expert"),
        P("shard", None),
        P("shard", None),
        P("expert", None, "shard"),
        P("expert", None, "shard"),
        P("expert", "shard", None),
    )
    out_specs = P("shard", "expert")
    return jax.shard_map(shards, mesh=mesh, in_specs=in_specs, out_specs=out_specs, check_vma=False)
```

profile of v0, /device:TPU:0, one launch (start us, length us, event | category | flops | bytes accessed | tf_op | source)
XLA Modules:
  0.0 105.6 jit_solution(6960518200582428909)
XLA Ops:
  0.0 0.7 convert_reduce_fusion
  0.7 0.2 reduce_window_sum.11
  0.9 6.4 %all_gather.9 = bf16[6,4096]{1,0:T(8,128)(2,1)S(1)} all-gather(bf16[6,1024]{1,0:T(8,128)(2,1)} %param.6), channel_id=1, replica_groups=mesh['expert'=4,'shard'=8] {'expert'}, dimensions={1}, use_global_device_ids=true | all-gather | bytes 61440 | tf_op jit(solution)/shard_map/all_gather | solution.py:20
  7.3 0.1 fusion.6
  7.5 32.4 %all-gather = bf16[8,6,4096]{2,1,0:T(8,128)(2,1)S(1)} all-gather(bf16[1,6,4096]{2,1,0:T(8,128)(2,1)S(1)} %fusion.6), channel_id=1, replica_groups=mesh['expert'=4,'shard'=8] {'shard'}, dimensions={0}, use_global_device_ids=true | all-gather | bytes 442368 | tf_op jit(solution)/shard_map/all_gather | solution.py:26
  39.9 0.1 reshape.15
  40.0 0.0 slice-start
  40.0 5.1 %fusion.4 = f32[48,1024]{1,0:T(8,128)S(1)} fusion(bf16[48,4096]{1,0:T(8,128)(2,1)S(1)} %reshape.15, bf16[1,4096,1024]{2,1,0:T(8,128)(2,1)} %param.9), kind=kOutput, calls=%fused_computation.4 | convolution fusion | flops 402653184 | bytes 8978432 | tf_op jit(solution)/shard_map/dot_general | solution.py:27
  45.1 0.0 slice-start.1
  45.1 5.1 %fusion.10 = bf16[48,1024]{1,0:T(8,128)(2,1)S(1)} fusion(bf16[48,4096]{1,0:T(8,128)(2,1)S(1)} %reshape.15, bf16[1,4096,1024]{2,1,0:T(8,128)(2,1)} %param.10, f32[48,1024]{1,0:T(8,128)S(1)} %fusion.4), kind=kOutput, calls=%fused_computation.9 | convolution fusion | flops 402948096 | bytes 9076736 | tf_op jit(solution)/shard_map/dot_general | solution.py:28
  50.2 0.0 copy-start
  50.3 0.0 copy-start.1
  50.3 31.6 %all_gather.11 = bf16[48,8192]{1,0:T(8,128)(2,1)S(1)} all-gather(bf16[48,1024]{1,0:T(8,128)(2,1)S(1)} %fusion.10), channel_id=1, replica_groups=mesh['expert'=4,'shard'=8] {'shard'}, dimensions={1}, use_global_device_ids=true | all-gather | bytes 884736 | tf_op jit(solution)/shard_map/all_gather | solution.py:31
  81.9 0.0 slice-done
  81.9 0.0 slice-done.1
  81.9 2.6 %fusion.13 = bf16[48,512]{1,0:T(8,128)(2,1)S(1)} fusion(bf16[48,8192]{1,0:T(8,128)(2,1)S(1)} %all_gather.11, bf16[1,512,8192]{2,1,0:T(8,128)(2,1)S(1)} %bitcast.40), kind=kOutput, calls=%fused_computation.10 | convolution fusion | flops 402677760 | bytes 9224192 | tf_op jit(solution)/shard_map/dot_general | solution.py:30
  84.6 12.8 %all_to_all.32 = bf16[8,6,512]{2,1,0:T(8,128)(2,1)} all-to-all(bf16[8,6,512]{2,1,0:T(8,128)(2,1)S(1)} %all_to_all.24), channel_id=1, replica_groups=mesh['expert'=4,'shard'=8] {'shard'}, dimensions={0} | all-to-all | bytes 98304 | tf_op jit(solution)/shard_map/all_to_all | solution.py:36
  97.4 3.3 %all-to-all-start.1 = ((bf16[6,4,1024]{2,0,1:T(8,128)(2,1)}), bf16[6,4,1024]{2,0,1:T(8,128)(2,1)S(1)}, u32[]{:S(2)}, u32[]{:S(2)}) async-start(bf16[6,4,1024]{2,0,1:T(8,128)(2,1)} %bitcast.9), calls=%async_computation.1 | async-start | bytes 131072 | tf_op jit(solution)/shard_map/all_to_all | solution.py:39
  100.7 0.0 copy-done
  100.7 0.0 copy-done.1
  100.7 4.1 %all-to-all-done.1 = bf16[6,4,1024]{2,0,1:T(8,128)(2,1)S(1)} async-done(((bf16[6,4,1024]{2,0,1:T(8,128)(2,1)}), bf16[6,4,1024]{2,0,1:T(8,128)(2,1)S(1)}, u32[]{:S(2)}, u32[]{:S(2)}) %all-to-all-start.1) | async-done | bytes 49184 | tf_op jit(solution)/shard_map/all_to_all | solution.py:39
  104.8 0.8 fusion.16
  (6 shorter events, 0.1 us)
Async XLA Ops:
  40.0 41.9 %slice-start = ((s8[8388608]{0:T(1024)(128)(4,1)}), s8[4194304]{0:T(1024)(128)(4,1)S(1)}, s32[]{:S(2)}) async-start(s8[8388608]{0:T(1024)(128)(4,1)} %bitcast.39), calls=%async_computation.2 | async-start | bytes 8388608
  45.1 36.8 %slice-start.1 = ((s8[8388608]{0:T(1024)(128)(4,1)}), s8[4194304]{0:T(1024)(128)(4,1)S(1)}, s32[]{:S(2)}) async-start(s8[8388608]{0:T(1024)(128)(4,1)} %bitcast.39), calls=%async_computation.3 | async-start | bytes 8388608
  50.2 50.4 %copy-start = (s32[6,2]{0,1:T(2,128)S(1)}, s32[6,2]{0,1:T(2,128)}, u32[]{:S(2)}) copy-start(s32[6,2]{0,1:T(2,128)} %param.7) | copy-start | bytes 148
  50.3 50.4 %copy-start.1 = (f32[6,2]{0,1:T(2,128)S(1)}, f32[6,2]{0,1:T(2,128)}, u32[]{:S(2)}) copy-start(f32[6,2]{0,1:T(2,128)} %param.8) | copy-start | bytes 148
  97.4 7.4 %all-to-all-start.1 = ((bf16[6,4,1024]{2,0,1:T(8,128)(2,1)}), bf16[6,4,1024]{2,0,1:T(8,128)(2,1)S(1)}, u32[]{:S(2)}, u32[]{:S(2)}) async-start(bf16[6,4,1024]{2,0,1:T(8,128)(2,1)} %bitcast.9), calls=%async_computation.1 | async-start | bytes 131072 | tf_op jit(solution)/shard_map/all_to_all | solution.py:39
where the time goes:
time: 106 us
  blocking collectives  83.2 us (78%)
  matrix products  13.8 us (13%)
  waiting for transfers between devices  4.05 us (4%)
  starting transfers between devices  3.28 us (3%)
    all_gather x1, blocking collectives, shards(): piece = lax.all_gather(own_rows, 'shard', axis=0, tiled=True)  32.4 us
    all_gather x1, blocking collectives, shards(): lax.all_gather(hidden, 'shard', axis=1, tiled=True)  31.6 us
    all_to_all x1, blocking collectives, shards(): lax.all_to_all(out_columns.astype(jnp.bfloat16), 'shard', split_axis=0, c...  12.8 us
    all_gather x1, blocking collectives, shards(): whole = lax.all_gather(tokens, 'expert', axis=1, tiled=True)  6.44 us
    dot_general x1, matrix products, shards(): up_out = jnp.dot(piece, up_local, preferred_element_type=jnp.float32)  5.11 us
    dot_general x1, matrix products, shards(): gate_out = jnp.dot(piece, gate_local, preferred_element_type=jnp.float32)  5.1 us
    all_to_all x1, waiting for transfers between devices, shards(): lax.all_to_all(expert_out, 'expert', split_axis=1, concat_axis=0, tiled=T...  4.05 us
    all_to_all x1, starting transfers between devices, shards(): lax.all_to_all(expert_out, 'expert', split_axis=1, concat_axis=0, tiled=T...  3.28 us
  transfers between devices with their start and end apart: 1, of which 1 were waited for; matrix products, arithmetic and copies ran while one was open for 0% of the time, Pallas kernels for 0%

commit v1 on v0

--- a/solution.py
+++ b/solution.py
@@ -17,7 +17,7 @@
     slot_range = jnp.arange(capacity, dtype=jnp.int32)
     selector = (slot_rank.T[:, None, :] == slot_range[None, :, None]) & (routed.T[:, None, :] > 0)
     selector_bf = selector.astype(jnp.bfloat16)
-    whole = lax.all_gather(tokens, "expert", axis=1, tiled=True)
+    whole = jnp.concatenate(jax.lax.all_gather(tokens, "expert"), axis=1)
     own_select = lax.dynamic_index_in_dim(selector_bf, own_expert, 0, keepdims=False)
     own_rows = jnp.dot(own_select, whole, preferred_element_type=jnp.float32).astype(jnp.bfloat16)
     gate_local = gate_proj[0]

time: 106 us -> 106 us (level)
  no operation moved by 1% of the time
where the time goes in v1:
time: 106 us
  blocking collectives  83.2 us (78%)
  matrix products  13.8 us (13%)
  waiting for transfers between devices  4.05 us (4%)
  starting transfers between devices  3.28 us (3%)
    all_gather x1, blocking collectives, shards(): piece = lax.all_gather(own_rows, 'shard', axis=0, tiled=True)  32.4 us
    all_gather x1, blocking collectives, shards(): lax.all_gather(hidden, 'shard', axis=1, tiled=True)  31.6 us
    all_to_all x1, blocking collectives, shards(): lax.all_to_all(out_columns.astype(jnp.bfloat16), 'shard', split_axis=0, c...  12.8 us
    all_gather x1, blocking collectives, shards(): whole = jnp.concatenate(jax.lax.all_gather(tokens, 'expert'), axis=1)  6.44 us
    dot_general x1, matrix products, shards(): up_out = jnp.dot(piece, up_local, preferred_element_type=jnp.float32)  5.11 us
    dot_general x1, matrix products, shards(): gate_out = jnp.dot(piece, gate_local, preferred_element_type=jnp.float32)  5.1 us
    all_to_all x1, waiting for transfers between devices, shards(): lax.all_to_all(expert_out, 'expert', split_axis=1, concat_axis=0, tiled=T...  4.05 us
    all_to_all x1, starting transfers between devices, shards(): lax.all_to_all(expert_out, 'expert', split_axis=1, concat_axis=0, tiled=T...  3.28 us
  transfers between devices with their start and end apart: 1, of which 1 were waited for; matrix products, arithmetic and copies ran while one was open for 0% of the time, Pallas kernels for 0%

profile of v1, /device:TPU:0, one launch (start us, length us, event | category | flops | bytes accessed | tf_op | source)
XLA Modules:
  0.0 105.6 jit_solution(13652036368125125389)
XLA Ops:
  0.0 0.7 convert_reduce_fusion
  0.7 0.2 reduce_window_sum.11
  0.9 6.4 %all-gather.1 = bf16[4,6,1024]{2,1,0:T(8,128)(2,1)S(1)} all-gather(bf16[1,6,1024]{2,1,0:T(8,128)(2,1)} %bitcast.46), channel_id=2, replica_groups=mesh['expert'=4,'shard'=8] {'expert'}, dimensions={0}, use_global_device_ids=true | all-gather | bytes 61440 | tf_op jit(solution)/shard_map/all_gather | solution.py:20
  7.3 0.1 fusion.6
  7.5 32.4 %all-gather.2 = bf16[8,6,4096]{2,1,0:T(8,128)(2,1)S(1)} all-gather(bf16[1,6,4096]{2,1,0:T(8,128)(2,1)S(1)} %fusion.6), channel_id=1, replica_groups=mesh['expert'=4,'shard'=8] {'shard'}, dimensions={0}, use_global_device_ids=true | all-gather | bytes 442368 | tf_op jit(solution)/shard_map/all_gather | solution.py:26
  39.9 0.1 reshape.26
  40.0 0.0 slice-start
  40.0 5.1 %fusion.4 = f32[48,1024]{1,0:T(8,128)S(1)} fusion(bf16[48,4096]{1,0:T(8,128)(2,1)S(1)} %reshape.26, bf16[1,4096,1024]{2,1,0:T(8,128)(2,1)} %param.9), kind=kOutput, calls=%fused_computation.4 | convolution fusion | flops 402653184 | bytes 8978432 | tf_op jit(solution)/shard_map/dot_general | solution.py:27
  45.1 0.0 slice-start.1
  45.1 5.1 %fusion.10 = bf16[48,1024]{1,0:T(8,128)(2,1)S(1)} fusion(bf16[48,4096]{1,0:T(8,128)(2,1)S(1)} %reshape.26, bf16[1,4096,1024]{2,1,0:T(8,128)(2,1)} %param.10, f32[48,1024]{1,0:T(8,128)S(1)} %fusion.4), kind=kOutput, calls=%fused_computation.9 | convolution fusion | flops 402948096 | bytes 9076736 | tf_op jit(solution)/shard_map/dot_general | solution.py:28
  50.2 0.0 copy-start
  50.3 0.0 copy-start.1
  50.3 31.6 %all_gather.15 = bf16[48,8192]{1,0:T(8,128)(2,1)S(1)} all-gather(bf16[48,1024]{1,0:T(8,128)(2,1)S(1)} %fusion.10), channel_id=1, replica_groups=mesh['expert'=4,'shard'=8] {'shard'}, dimensions={1}, use_global_device_ids=true | all-gather | bytes 884736 | tf_op jit(solution)/shard_map/all_gather | solution.py:31
  81.9 0.0 slice-done
  81.9 0.0 slice-done.1
  81.9 2.6 %fusion.13 = bf16[48,512]{1,0:T(8,128)(2,1)S(1)} fusion(bf16[48,8192]{1,0:T(8,128)(2,1)S(1)} %all_gather.15, bf16[1,512,8192]{2,1,0:T(8,128)(2,1)S(1)} %bitcast.44), kind=kOutput, calls=%fused_computation.10 | convolution fusion | flops 402677760 | bytes 9224192 | tf_op jit(solution)/shard_map/dot_general | solution.py:30
  84.6 12.8 %all_to_all.32 = bf16[8,6,512]{2,1,0:T(8,128)(2,1)} all-to-all(bf16[8,6,512]{2,1,0:T(8,128)(2,1)S(1)} %all_to_all.24), channel_id=1, replica_groups=mesh['expert'=4,'shard'=8] {'shard'}, dimensions={0} | all-to-all | bytes 98304 | tf_op jit(solution)/shard_map/all_to_all | solution.py:36
  97.4 3.3 %all-to-all-start.1 = ((bf16[6,4,1024]{2,0,1:T(8,128)(2,1)}), bf16[6,4,1024]{2,0,1:T(8,128)(2,1)S(1)}, u32[]{:S(2)}, u32[]{:S(2)}) async-start(bf16[6,4,1024]{2,0,1:T(8,128)(2,1)} %bitcast.12), calls=%async_computation.1 | async-start | bytes 131072 | tf_op jit(solution)/shard_map/all_to_all | solution.py:39
  100.7 0.0 copy-done
  100.7 0.0 copy-done.1
  100.7 4.1 %all-to-all-done.1 = bf16[6,4,1024]{2,0,1:T(8,128)(2,1)S(1)} async-done(((bf16[6,4,1024]{2,0,1:T(8,128)(2,1)}), bf16[6,4,1024]{2,0,1:T(8,128)(2,1)S(1)}, u32[]{:S(2)}, u32[]{:S(2)}) %all-to-all-start.1) | async-done | bytes 49184 | tf_op jit(solution)/shard_map/all_to_all | solution.py:39
  104.8 0.8 fusion.16
  (6 shorter events, 0.1 us)
Async XLA Ops:
  40.0 41.9 %slice-start = ((s8[8388608]{0:T(1024)(128)(4,1)}), s8[4194304]{0:T(1024)(128)(4,1)S(1)}, s32[]{:S(2)}) async-start(s8[8388608]{0:T(1024)(128)(4,1)} %bitcast.43), calls=%async_computation.2 | async-start | bytes 8388608
  45.1 36.8 %slice-start.1 = ((s8[8388608]{0:T(1024)(128)(4,1)}), s8[4194304]{0:T(1024)(128)(4,1)S(1)}, s32[]{:S(2)}) async-start(s8[8388608]{0:T(1024)(128)(4,1)} %bitcast.43), calls=%async_computation.3 | async-start | bytes 8388608
  50.2 50.4 %copy-start = (s32[6,2]{0,1:T(2,128)S(1)}, s32[6,2]{0,1:T(2,128)}, u32[]{:S(2)}) copy-start(s32[6,2]{0,1:T(2,128)} %param.7) | copy-start | bytes 148
  50.3 50.4 %copy-start.1 = (f32[6,2]{0,1:T(2,128)S(1)}, f32[6,2]{0,1:T(2,128)}, u32[]{:S(2)}) copy-start(f32[6,2]{0,1:T(2,128)} %param.8) | copy-start | bytes 148
  97.4 7.4 %all-to-all-start.1 = ((bf16[6,4,1024]{2,0,1:T(8,128)(2,1)}), bf16[6,4,1024]{2,0,1:T(8,128)(2,1)S(1)}, u32[]{:S(2)}, u32[]{:S(2)}) async-start(bf16[6,4,1024]{2,0,1:T(8,128)(2,1)} %bitcast.12), calls=%async_computation.1 | async-start | bytes 131072 | tf_op jit(solution)/shard_map/all_to_all | solution.py:39
